TPU v7x, 32 devices: a whole 2x2x4 slice. The times are simulated.
32 devices in a mesh: group: 4 (over y, core), replica: 8 (over z, x).
Axes of the slice: x: 2, y: 2, z: 4, core: 2. Of those that a mesh axis runs over, the one named last changes fastest.
Arguments:
- inputs: bfloat16 [32, 128, 1600], P(('group', 'replica')), may hold values from -6 to 6
- segments: int32 [32, 128], P(('group', 'replica')), may hold values from 0 to 3, never falling along the last dimension, each value on 1 to 64 neighbouring positions
- cotangent: bfloat16 [32, 128, 1600], P(('group', 'replica')), may hold values from -6 to 6
- norm1_gain: bfloat16 [1600], P('group'), may hold values from 0.5 to 1.5
- norm1_bias: bfloat16 [1600], P('group'), may hold values from -3 to 3
- w_qkv: bfloat16 [1600, 4800], P('group'), may hold values from -8 to 8
- bias_qv: bfloat16 [3200], P('group'), may hold values from -3 to 3
- w_out: bfloat16 [1600, 1600], P('group'), may hold values from -0.625 to 0.625
- bias_out: bfloat16 [1600], P('group'), may hold values from -3 to 3
- norm2_gain: bfloat16 [1600], P('group'), may hold values from 0.5 to 1.5
- norm2_bias: bfloat16 [1600], P('group'), may hold values from -3 to 3
- w_fc: bfloat16 [1600, 6400], P('group'), may hold values from -0.15625 to 0.15625
- bias_fc: bfloat16 [6400], P('group'), may hold values from -3 to 3
- w_proj: bfloat16 [6400, 1600], P('group'), may hold values from -0.078125 to 0.078125
- bias_proj: bfloat16 [1600], P('group'), may hold values from -3 to 3
Outputs:
- outputs: bfloat16 [32, 128, 1600], P(('group', 'replica'))
- input_grad: float32 [32, 128, 1600], P(('group', 'replica'))
- grad_norm1_gain: float32 [1600], P('group')
- grad_norm1_bias: float32 [1600], P('group')
- grad_w_qkv: float32 [1600, 4800], P('group')
- grad_bias_qv: float32 [3200], P('group')
- grad_w_out: float32 [1600, 1600], P('group')
- grad_bias_out: float32 [1600], P('group')
- grad_norm2_gain: float32 [1600], P('group')
- grad_norm2_bias: float32 [1600], P('group')
- grad_w_fc: float32 [1600, 6400], P('group')
- grad_bias_fc: float32 [6400], P('group')
- grad_w_proj: float32 [6400, 1600], P('group')
- grad_bias_proj: float32 [1600], P('group')
Inputs may be any that keep to these rules, and one draw needn't show every extreme that they name: `segments`: each packed row's segment numbers never fall; a segment holds 1 to 64 tokens, and some segment holds exactly that many.
All inputs are finite; a program needn't handle non-finite values.
Results may differ from a plain program's by a relative error of at most 0.0095.
Values may be sent and summed in bfloat16 or wider, within the bound.
A program may use at most 640 MiB of HBM per device.

v0:
```python
import jax
import jax.numpy as jnp
from jax import lax
from jax.sharding import PartitionSpec as P

HEAD_DIM = 64
EPSILON = 1e-05
GELU_SCALE = 0.7978845608028654
CUBIC_TERM = 0.044715


def matmul_plain(left_side, right_side):
    return jnp.dot(left_side, right_side, preferred_element_type=jnp.float32)


def matmul_left(left_side, right_side):
    return lax.dot_general(
        left_side, right_side, (((0,), (0,)), ((), ())), preferred_element_type=jnp.float32
    )


def matmul_right(left_side, right_side):
    return lax.dot_general(
        left_side, right_side, (((1,), (1,)), ((), ())), preferred_element_type=jnp.float32
    )


def batched(form, left_side, right_side):
    return jnp.einsum(form, left_side, right_side, preferred_element_type=jnp.float32)


def norm_forward(values, norm_gain, offset):
    center = values - jnp.mean(values, axis=-1, keepdims=True)
    inverse = lax.rsqrt(jnp.mean(center * center, axis=-1, keepdims=True) + EPSILON)
    scaled = center * inverse
    return (scaled * norm_gain + offset, scaled, inverse)


def norm_backward(upstream, scaled, inverse, norm_gain):
    weighted = upstream * norm_gain
    result = inverse * (
        weighted
        - jnp.mean(weighted, axis=-1, keepdims=True)
        - scaled * jnp.mean(weighted * scaled, axis=-1, keepdims=True)
    )
    return (result, jnp.sum(upstream * scaled, axis=0), jnp.sum(upstream, axis=0))


def gelu_tanh(values):
    tangent = jnp.tanh(GELU_SCALE * (values + CUBIC_TERM * values * values * values))
    return 0.5 * values * (1.0 + tangent)


def gelu_slope(values):
    tangent = jnp.tanh(GELU_SCALE * (values + CUBIC_TERM * values * values * values))
    return 0.5 * (1.0 + tangent) + 0.5 * values * (1.0 - tangent * tangent) * GELU_SCALE * (
        1.0 + 3.0 * CUBIC_TERM * values * values
    )


def allowed_mask(segments):
    positions = jnp.arange(segments.shape[1])
    causal = positions[:, None] >= positions[None, :]
    same_segment = segments[:, :, None] == segments[:, None, :]
    return (same_segment & causal[None, :, :])[:, None, :, :]


def masked_scores(queries, keyed, allowed):
    raw = batched("rqhd,rkhd->rhqk", queries, keyed) * HEAD_DIM ** (-0.5)
    return jnp.where(allowed, raw, -1e30)


def layer_forward(inputs, segments, params):
    (
        norm1_gain,
        norm1_bias,
        w_qkv,
        bias_qv,
        w_out,
        bias_out,
        norm2_gain,
        norm2_bias,
        w_fc,
        bias_fc,
        w_proj,
        bias_proj,
    ) = params
    row_count, length, feature_width = inputs.shape
    head_count = feature_width // HEAD_DIM
    tokens = inputs.reshape(row_count * length, feature_width).astype(jnp.float32)
    first_norm, first_scaled, first_inverse = norm_forward(
        tokens, norm1_gain.astype(jnp.float32), norm1_bias.astype(jnp.float32)
    )
    first_cast = first_norm.astype(jnp.bfloat16)
    qkv_bias = jnp.concatenate(
        [
            bias_qv[:feature_width].astype(jnp.float32),
            jnp.zeros((feature_width,), jnp.float32),
            bias_qv[feature_width:].astype(jnp.float32),
        ]
    )
    projected = (matmul_plain(first_cast, w_qkv) + qkv_bias).astype(jnp.bfloat16)
    split_qkv = projected.reshape(row_count, length, 3, head_count, HEAD_DIM)
    queries, keyed, values = (split_qkv[:, :, 0], split_qkv[:, :, 1], split_qkv[:, :, 2])
    allowed = allowed_mask(segments)
    scores = masked_scores(queries, keyed, allowed)
    row_peak = jnp.max(scores, axis=-1, keepdims=True)
    logsum = row_peak + jnp.log(jnp.sum(jnp.exp(scores - row_peak), axis=-1, keepdims=True))
    attn_probs = jnp.exp(scores - logsum).astype(jnp.bfloat16)
    attended = batched("rhqk,rkhd->rqhd", attn_probs, values).reshape(
        row_count * length, feature_width
    )
    attended_cast = attended.astype(jnp.bfloat16)
    residual = tokens + matmul_plain(attended_cast, w_out) + bias_out.astype(jnp.float32)
    second_norm, second_scaled, second_inverse = norm_forward(
        residual, norm2_gain.astype(jnp.float32), norm2_bias.astype(jnp.float32)
    )
    second_cast = second_norm.astype(jnp.bfloat16)
    hidden_pre = matmul_plain(second_cast, w_fc) + bias_fc.astype(jnp.float32)
    hidden = gelu_tanh(hidden_pre).astype(jnp.bfloat16)
    result = residual + matmul_plain(hidden, w_proj) + bias_proj.astype(jnp.float32)
    outputs = result.astype(jnp.bfloat16).reshape(row_count, length, feature_width)
    stored = (
        first_scaled,
        first_inverse,
        first_cast,
        projected,
        logsum,
        attended,
        attended_cast,
        second_scaled,
        second_inverse,
        second_cast,
        hidden_pre,
        hidden,
        allowed,
    )
    return (outputs, stored)


def layer_backward(cotangent, params, stored):
    (
        norm1_gain,
        norm1_bias,
        w_qkv,
        bias_qv,
        w_out,
        bias_out,
        norm2_gain,
        norm2_bias,
        w_fc,
        bias_fc,
        w_proj,
        bias_proj,
    ) = params
    (
        first_scaled,
        first_inverse,
        first_cast,
        projected,
        logsum,
        attended,
        attended_cast,
        second_scaled,
        second_inverse,
        second_cast,
        hidden_pre,
        hidden,
        allowed,
    ) = stored
    row_count, length, feature_width = cotangent.shape
    head_count = feature_width // HEAD_DIM
    token_count = row_count * length
    upstream_cast = cotangent.reshape(token_count, feature_width)
    upstream = upstream_cast.astype(jnp.float32)
    grad_w_proj = matmul_left(hidden, upstream_cast)
    grad_bias_proj = jnp.sum(upstream, axis=0)
    grad_hidden = matmul_right(upstream_cast, w_proj) * gelu_slope(hidden_pre)
    grad_hidden_cast = grad_hidden.astype(jnp.bfloat16)
    grad_w_fc = matmul_left(second_cast, grad_hidden_cast)
    grad_bias_fc = jnp.sum(grad_hidden, axis=0)
    second_back, grad_norm2_gain, grad_norm2_bias = norm_backward(
        matmul_right(grad_hidden_cast, w_fc),
        second_scaled,
        second_inverse,
        norm2_gain.astype(jnp.float32),
    )
    grad_residual = upstream + second_back
    grad_residual_cast = grad_residual.astype(jnp.bfloat16)
    grad_w_out = matmul_left(attended_cast, grad_residual_cast)
    grad_bias_out = jnp.sum(grad_residual, axis=0)
    grad_attended = (
        matmul_right(grad_residual_cast, w_out)
        .astype(jnp.bfloat16)
        .reshape(row_count, length, head_count, HEAD_DIM)
    )
    split_qkv = projected.reshape(row_count, length, 3, head_count, HEAD_DIM)
    queries, keyed, values = (split_qkv[:, :, 0], split_qkv[:, :, 1], split_qkv[:, :, 2])
    scores = masked_scores(queries, keyed, allowed)
    exact_probs = jnp.exp(scores - logsum)
    attn_probs = exact_probs.astype(jnp.bfloat16)
    grad_probs = batched("rqhd,rkhd->rhqk", grad_attended, values)
    row_delta = jnp.sum(
        grad_attended.astype(jnp.float32)
        * attended.reshape(row_count, length, head_count, HEAD_DIM),
        axis=-1,
    )
    row_delta = jnp.transpose(row_delta, (0, 2, 1))[:, :, :, None]
    grad_scores = (exact_probs * (grad_probs - row_delta) * HEAD_DIM ** (-0.5)).astype(jnp.bfloat16)
    grad_queries = batched("rhqk,rkhd->rqhd", grad_scores, keyed)
    grad_keyed = batched("rhqk,rqhd->rkhd", grad_scores, queries)
    grad_values = batched("rhqk,rqhd->rkhd", attn_probs, grad_attended)
    grad_projected = jnp.stack([grad_queries, grad_keyed, grad_values], axis=2).reshape(
        token_count, 3 * feature_width
    )
    grad_bias_qv = jnp.concatenate(
        [
            jnp.sum(grad_projected[:, :feature_width], axis=0),
            jnp.sum(grad_projected[:, 2 * feature_width :], axis=0),
        ]
    )
    grad_projected_cast = grad_projected.astype(jnp.bfloat16)
    grad_w_qkv = matmul_left(first_cast, grad_projected_cast)
    first_back, grad_norm1_gain, grad_norm1_bias = norm_backward(
        matmul_right(grad_projected_cast, w_qkv),
        first_scaled,
        first_inverse,
        norm1_gain.astype(jnp.float32),
    )
    input_grad = (grad_residual + first_back).reshape(row_count, length, feature_width)
    grads = (
        grad_norm1_gain,
        grad_norm1_bias,
        grad_w_qkv,
        grad_bias_qv,
        grad_w_out,
        grad_bias_out,
        grad_norm2_gain,
        grad_norm2_bias,
        grad_w_fc,
        grad_bias_fc,
        grad_w_proj,
        grad_bias_proj,
    )
    return (input_grad, grads)


def per_device(
    inputs,
    segments,
    cotangent,
    norm1_gain,
    norm1_bias,
    w_qkv,
    bias_qv,
    w_out,
    bias_out,
    norm2_gain,
    norm2_bias,
    w_fc,
    bias_fc,
    w_proj,
    bias_proj,
):
    forward_params = (
        lax.all_gather(norm1_gain, "group", axis=0, tiled=True),
        lax.all_gather(norm1_bias, "group", axis=0, tiled=True),
        lax.all_gather(w_qkv, "group", axis=0, tiled=True),
        lax.all_gather(bias_qv, "group", axis=0, tiled=True),
        lax.all_gather(w_out, "group", axis=0, tiled=True),
        lax.all_gather(bias_out, "group", axis=0, tiled=True),
        lax.all_gather(norm2_gain, "group", axis=0, tiled=True),
        lax.all_gather(norm2_bias, "group", axis=0, tiled=True),
        lax.all_gather(w_fc, "group", axis=0, tiled=True),
        lax.all_gather(bias_fc, "group", axis=0, tiled=True),
        lax.all_gather(w_proj, "group", axis=0, tiled=True),
        lax.all_gather(bias_proj, "group", axis=0, tiled=True),
    )
    outputs, stored = layer_forward(inputs, segments, forward_params)
    backward_params = (
        lax.all_gather(norm1_gain, "group", axis=0, tiled=True),
        lax.all_gather(norm1_bias, "group", axis=0, tiled=True),
        lax.all_gather(w_qkv, "group", axis=0, tiled=True),
        lax.all_gather(bias_qv, "group", axis=0, tiled=True),
        lax.all_gather(w_out, "group", axis=0, tiled=True),
        lax.all_gather(bias_out, "group", axis=0, tiled=True),
        lax.all_gather(norm2_gain, "group", axis=0, tiled=True),
        lax.all_gather(norm2_bias, "group", axis=0, tiled=True),
        lax.all_gather(w_fc, "group", axis=0, tiled=True),
        lax.all_gather(bias_fc, "group", axis=0, tiled=True),
        lax.all_gather(w_proj, "group", axis=0, tiled=True),
        lax.all_gather(bias_proj, "group", axis=0, tiled=True),
    )
    input_grad, grads = layer_backward(cotangent, backward_params, stored)
    owned = (
        lax.psum_scatter(grads[0], "group", scatter_dimension=0, tiled=True),
        lax.psum_scatter(grads[1], "group", scatter_dimension=0, tiled=True),
        lax.psum_scatter(grads[2], "group", scatter_dimension=0, tiled=True),
        lax.psum_scatter(grads[3], "group", scatter_dimension=0, tiled=True),
        lax.psum_scatter(grads[4], "group", scatter_dimension=0, tiled=True),
        lax.psum_scatter(grads[5], "group", scatter_dimension=0, tiled=True),
        lax.psum_scatter(grads[6], "group", scatter_dimension=0, tiled=True),
        lax.psum_scatter(grads[7], "group", scatter_dimension=0, tiled=True),
        lax.psum_scatter(grads[8], "group", scatter_dimension=0, tiled=True),
        lax.psum_scatter(grads[9], "group", scatter_dimension=0, tiled=True),
        lax.psum_scatter(grads[10], "group", scatter_dimension=0, tiled=True),
        lax.psum_scatter(grads[11], "group", scatter_dimension=0, tiled=True),
    )
    summed = lax.psum(
        (
            owned[0],
            owned[1],
            owned[2],
            owned[3],
            owned[4],
            owned[5],
            owned[6],
            owned[7],
            owned[8],
            owned[9],
            owned[10],
            owned[11],
        ),
        "replica",
    )
    return (
        outputs,
        input_grad,
        summed[0],
        summed[1],
        summed[2],
        summed[3],
        summed[4],
        summed[5],
        summed[6],
        summed[7],
        summed[8],
        summed[9],
        summed[10],
        summed[11],
    )


def solution(mesh):
    return jax.shard_map(
        per_device,
        mesh=mesh,
        in_specs=(
            P(("group", "replica"), None, None),
            P(("group", "replica"), None),
            P(("group", "replica"), None, None),
            P("group"),
            P("group"),
            P("group", None),
            P("group"),
            P("group", None),
            P("group"),
            P("group"),
            P("group"),
            P("group", None),
            P("group"),
            P("group", None),
            P("group"),
        ),
        out_specs=(
            P(("group", "replica"), None, None),
            P(("group", "replica"), None, None),
            P("group"),
            P("group"),
            P("group", None),
            P("group"),
            P("group", None),
            P("group"),
            P("group"),
            P("group"),
            P("group", None),
            P("group"),
            P("group", None),
            P("group"),
        ),
        check_vma=False,
    )
```

profile of v0, /device:TPU:0, one launch (start us, length us, event | category | flops | bytes accessed | tf_op | source)
XLA Modules:
  0.0 2333.0 jit_solution(5948088002728456721)
XLA Ops:
  7.2 0.7 all-gather.5.cloned.1.call-update
  8.0 0.7 all-gather.7.cloned.1.call-update
  14.8 14.5 all-reduce.19
  30.1 81.4 %all-gather.5.cloned.1.call-done = bf16[1600,4800]{1,0:T(8,128)(2,1)} async-done(((bf16[400,4800]{1,0:T(8,128)(2,1)}), bf16[1600,4800]{1,0:T(8,128)(2,1)}) %all-gather.5.cloned.1.call-update) | async-done | bytes 15360016 | tf_op jit(solution)/shard_map/all_gather | solution.py:268
  111.5 13.2 fusion
  124.6 1.6 fusion.62
  126.5 2.3 fusion.63
  128.8 25.2 %all-gather.7.cloned.1.call-done = bf16[1600,1600]{1,0:T(8,128)(2,1)} async-done(((bf16[400,1600]{1,0:T(8,128)(2,1)}), bf16[1600,1600]{1,0:T(8,128)(2,1)}) %all-gather.7.cloned.1.call-update) | async-done | bytes 5120016 | tf_op jit(solution)/shard_map/all_gather | solution.py:270
  154.0 4.8 fusion.64
  159.0 125.5 %all-gather.9.cloned.1.call-done = bf16[1600,6400]{1,0:T(8,128)(2,1)} async-done(((bf16[400,6400]{1,0:T(8,128)(2,1)}), bf16[1600,6400]{1,0:T(8,128)(2,1)}) %all-gather.9.cloned.1.call-update) | async-done | bytes 20480016 | tf_op jit(solution)/shard_map/all_gather | solution.py:274
  284.5 12.4 convolution_add_fusion
  296.9 122.5 %all-gather.11.cloned.1.call-done = bf16[6400,1600]{1,0:T(8,128)(2,1)} async-done(((bf16[1600,1600]{1,0:T(8,128)(2,1)}), bf16[6400,1600]{1,0:T(8,128)(2,1)}) %all-gather.11.cloned.1.call-update) | async-done | bytes 20480016 | tf_op jit(solution)/shard_map/all_gather | solution.py:276
  419.4 12.0 fusion.65
  431.4 12.7 multiply_reduce_fusion
  444.1 1.3 fusion.60
  445.4 0.9 copy-done.1
  446.3 5.7 fusion.55
  452.3 4.4 convolution_convert_fusion
  458.5 0.7 convolution_bitcast_fusion
  459.2 0.9 copy-done.5
  460.4 15.0 fusion.39
  475.5 1.4 copy-done.4
  476.9 16.5 fusion.34
  494.4 18.8 fusion.42
  513.3 1.1 copy-done.6
  514.6 1.4 pad_maximum_fusion
  517.2 9.8 fusion.27
  527.1 10.5 reduce-scatter.7.cloned.1.call-done
  537.6 224.2 %reduce-scatter.5.cloned.1.call-done = f32[400,4800]{1,0:T(8,128)} async-done(((f32[1600,4800]{1,0:T(8,128)}), f32[400,4800]{1,0:T(8,128)}) %reduce-scatter.5.cloned.1.call-update) | async-done | bytes 7680016 | tf_op jit(solution)/shard_map/reduce_scatter | solution.py:298
  761.8 295.6 %reduce-scatter.9.cloned.1.call-done = f32[400,6400]{1,0:T(8,128)} async-done(((f32[1600,6400]{1,0:T(8,128)}), f32[400,6400]{1,0:T(8,128)}) %reduce-scatter.9.cloned.1.call-update) | async-done | bytes 10240016 | tf_op jit(solution)/shard_map/reduce_scatter | solution.py:304
  1057.4 289.3 %reduce-scatter.11.cloned.1.call-done = f32[1600,1600]{1,0:T(8,128)} async-done(((f32[6400,1600]{1,0:T(8,128)}), f32[1600,1600]{1,0:T(8,128)}) %reduce-scatter.11.cloned.1.call-update) | async-done | bytes 10240016 | tf_op jit(solution)/shard_map/reduce_scatter | solution.py:306
  1348.8 1.2 fusion.26
  1350.0 14.8 fusion.9
  1364.8 18.3 all-reduce.25.cloned.1.call-done
  1383.1 0.8 dynamic-slice.9
  1383.8 0.8 dynamic-slice.11
  1384.6 0.8 dynamic-slice.15
  1385.4 0.8 dynamic-slice.17
  1386.2 0.8 dynamic-slice.19
  1386.9 0.8 dynamic-slice.23
  1387.7 0.8 dynamic-slice.13
  1388.5 0.8 dynamic-slice.21
  1389.2 39.9 %all-reduce.16 = (f32[400]{0:T(512)}, f32[400]{0:T(512)}, f32[800]{0:T(1024)}, f32[400]{0:T(512)}, f32[400]{0:T(512)}, /*index=5*/f32[400]{0:T(512)}, f32[1600]{0:T(1024)}, f32[400]{0:T(512)}) all-reduce(f32[400]{0:T(512)S(1)} %dynamic-slice.9, f32[400]{0:T(512)S(1)} %dynamic-slice.11, ...), channel_id=1, replica_groups=mesh['group'=4,'replica'=8] {'replica'}, use_global_device_ids=true, to_apply=%region_13.14 | all-reduce | flops 4800 | bytes 38400 | tf_op jit(solution)/shard_map/psum | solution.py:309
  1429.2 874.7 %all-reduce.23.cloned.1.call-done = (f32[400,4800]{1,0:T(8,128)}, f32[400,1600]{1,0:T(8,128)}, f32[400,6400]{1,0:T(8,128)}, f32[1600,1600]{1,0:T(8,128)}) async-done(((f32[400,4800]{1,0:T(8,128)}, f32[400,1600]{1,0:T(8,128)}, f32[400,6400]{1,0:T(8,128)}, f32[1600,1600]{1,0:T(8,128)}), (f32[400,4800]{1,0:T(8,128)}, f32[400,1600]{1,0:T(8,128)}, f32[400,6400]{1,0:T(8,128)}, ...) | async-done | bytes 30720016 | tf_op jit(solution)/shard_map/psum | solution.py:309
  2303.9 7.1 copy.64
  2310.9 1.5 copy.65
  2312.4 9.3 copy.66
  2321.7 4.1 copy.67
  (118 shorter events, 10.4 us)
Async XLA Ops:
  7.2 104.3 %all-gather.5.cloned.1.call-start = ((), (), s32[]{:S(2)}) async-start(), calls=%async_computation.4 | async-start | bytes 19456000 | tf_op jit(solution)/shard_map/all_gather | solution.py:268
  7.9 146.1 %all-gather.7.cloned.1.call-start = ((), (), s32[]{:S(2)}) async-start(), calls=%async_computation.5 | async-start | bytes 6656000 | tf_op jit(solution)/shard_map/all_gather | solution.py:270
  8.7 275.9 %all-gather.9.cloned.1.call-start = ((), (), s32[]{:S(2)}) async-start(), calls=%async_computation.6 | async-start | bytes 25600000 | tf_op jit(solution)/shard_map/all_gather | solution.py:274
  9.4 0.7 copy-start.17
  9.4 3.3 copy-start.19
  9.4 3.5 copy-start.20
  9.4 3.8 copy-start.21
  9.4 4.0 copy-start.22
  9.5 4.3 copy-start.23
  9.5 4.5 copy-start.24
  9.5 4.8 copy-start.18
  9.5 5.0 copy-start.15
  9.5 20.0 copy-start
  9.5 20.5 copy-start.16
  9.5 409.9 %all-gather.11.cloned.1.call-start = ((), (), s32[]{:S(2)}) async-start(), calls=%async_computation.7 | async-start | bytes 26624000 | tf_op jit(solution)/shard_map/all_gather | solution.py:276
  10.1 527.5 %reduce-scatter.7.cloned.1.call-start = ((), (), s32[]{:S(2)}) async-start(), calls=%async_computation.9 | async-start | bytes 13312000 | tf_op jit(solution)/shard_map/reduce_scatter | solution.py:300
  431.4 12.7 copy-start.3
  431.4 12.7 copy-start.13
  445.4 0.9 copy-start.1
  452.0 309.8 %reduce-scatter.5.cloned.1.call-start = ((), (), s32[]{:S(2)}) async-start(), calls=%async_computation.8 | async-start | bytes 38912000 | tf_op jit(solution)/shard_map/reduce_scatter | solution.py:298
  452.3 4.4 copy-start.11
  452.3 4.6 copy-start.10
  458.1 2.2 copy-start.7
  458.5 1.9 copy-start.9
  459.2 0.9 copy-start.5
  475.4 1.5 copy-start.4
  475.4 582.0 %reduce-scatter.9.cloned.1.call-start = ((), (), s32[]{:S(2)}) async-start(), calls=%async_computation.10 | async-start | bytes 51200000 | tf_op jit(solution)/shard_map/reduce_scatter | solution.py:304
  493.4 1.0 copy-start.14
  493.4 853.3 %reduce-scatter.11.cloned.1.call-start = ((), (), s32[]{:S(2)}) async-start(), calls=%async_computation.11 | async-start | bytes 53248000 | tf_op jit(solution)/shard_map/reduce_scatter | solution.py:306
  513.2 1.1 copy-start.6
  513.2 1.4 copy-start.8
  513.2 869.8 %all-reduce.25.cloned.1.call-start = ((), (), s32[]{:S(2)}) async-start(), calls=%async_computation.13 | async-start | bytes 188416
  527.0 1776.8 %all-reduce.23.cloned.1.call-start = ((), (), s32[]{:S(2)}) async-start(), calls=%async_computation.12 | async-start | bytes 62668800 | tf_op jit(solution)/shard_map/psum | solution.py:309
  1346.7 2.1 copy-start.2
  2303.9 7.1 copy-start.12
  2310.9 10.8 slice-start
  2312.4 9.3 slice-start.1
  2312.4 9.3 slice-start.2
Sparse Core Ops, SparseCore 0:
  9.5 101.8 all-gather.4
  113.0 40.9 all-gather.6
  155.6 128.8 all-gather.8
  285.9 133.3 all-gather.10
  452.1 85.4 reduce-scatter.6
  540.1 221.6 reduce-scatter.4
  764.4 292.9 reduce-scatter.8
  1060.0 286.6 reduce-scatter.10
  1350.7 32.3 all-reduce.24
  1387.8 916.0 all-reduce.22
where the time goes:
time: 2340 us; the launch traced here: 2330 us
  waiting for transfers between devices  2070 us (88%)
  matrix products  146 us (6%)
  blocking collectives  54.4 us (2%)
  local copies, waits for them, and re-layouts  36.2 us (2%)
    psum x1, waiting for transfers between devices, per_device(): lax.psum((owned[0], owned[1], owned[2], owned[3], owned[4], owned[5], own...  875 us
    reduce_scatter x1, waiting for transfers between devices, per_device(): lax.psum_scatter(grads[8], 'group', scatter_dimension=0, tiled=True)  296 us
    reduce_scatter x1, waiting for transfers between devices, per_device(): lax.psum_scatter(grads[10], 'group', scatter_dimension=0, tiled=True)  289 us
    reduce_scatter x1, waiting for transfers between devices, per_device(): lax.psum_scatter(grads[2], 'group', scatter_dimension=0, tiled=True)  224 us
    all_gather x1, waiting for transfers between devices, per_device(): lax.all_gather(w_fc, 'group', axis=0, tiled=True)  125 us
    all_gather x1, waiting for transfers between devices, per_device(): lax.all_gather(w_proj, 'group', axis=0, tiled=True)  122 us
    all_gather x1, waiting for transfers between devices, per_device(): lax.all_gather(w_qkv, 'group', axis=0, tiled=True)  81.4 us
    dot_general x4, matrix products, matmul_left(): lax.dot_general(left_side, right_side, (((0,), (0,)), ((), ())), preferre...  56 us
  transfers between devices with their start and end apart: 10, of which 10 were waited for; matrix products, arithmetic and copies ran while one was open for 6% of the time, Pallas kernels for 0%

commit v1 on v0

--- a/solution.py
+++ b/solution.py
@@ -7,6 +7,32 @@
 EPSILON = 1e-05
 GELU_SCALE = 0.7978845608028654
 CUBIC_TERM = 0.044715
+
+
+def process_sample(sample, along_dim):
+    far_arr = list(sample.shape[1:])
+    far_arr[along_dim] *= sample.shape[0]
+    a_now = jnp.moveaxis(sample, 0, along_dim).reshape(far_arr)
+    return a_now
+
+
+def _spread_yards(xx, axis_tag, array_axis):
+    chips = lax.axis_size(axis_tag)
+    nodes = [(jj, (jj + 1) % chips) for jj in range(chips)]
+    met_up, z2 = ([], [])
+    buffers = [(no, p) for p, no in nodes]
+    for tick in range(chips - 1):
+        if tick % 2 == 0:
+            met_up.append(
+                lax.ppermute(met_up[-1] if met_up else xx, axis_name=axis_tag, perm=nodes)
+            )
+        else:
+            z2.append(lax.ppermute(z2[-1] if z2 else xx, axis_name=axis_tag, perm=buffers))
+    vec_out = jnp.stack([*met_up[::-1], xx, *z2])
+    step_out = lax.axis_index(axis_tag) - len(met_up)
+    vec_out = vec_out[(jnp.arange(chips) - step_out) % chips]
+    local_now = process_sample(vec_out, array_axis)
+    return local_now
 
 
 def matmul_plain(left_side, right_side):
@@ -271,7 +297,7 @@
         lax.all_gather(bias_out, "group", axis=0, tiled=True),
         lax.all_gather(norm2_gain, "group", axis=0, tiled=True),
         lax.all_gather(norm2_bias, "group", axis=0, tiled=True),
-        lax.all_gather(w_fc, "group", axis=0, tiled=True),
+        _spread_yards(w_fc, "group", 0),
         lax.all_gather(bias_fc, "group", axis=0, tiled=True),
         lax.all_gather(w_proj, "group", axis=0, tiled=True),
         lax.all_gather(bias_proj, "group", axis=0, tiled=True),

time: 2340 us -> 2450 us (1.047)
  blocking collectives: 54.4 us -> 168 us
  waiting for transfers between devices: 2070 us -> 1990 us
  other arithmetic: 6.75 us -> 40.1 us
  local copies, waits for them, and re-layouts: 36.2 us -> 63.4 us
    ppermute x0 -> x3, waiting for transfers between devices: none -> 192 us  [the longest x2 192 us: _spread_yards(): lax.ppermute(met_up[-1] if met_up else xx, axis_name=axis_tag, perm=nodes)]
    all_gather x1, waiting for transfers between devices: 122 us -> 0.01 us  [per_device(): lax.all_gather(w_proj, 'group', axis=0, tiled=True)]
    unnamed x1, blocking collectives: 14.5 us -> 129 us
    all_gather x1, waiting for transfers between devices: 81.4 us -> 0.02 us  [per_device(): lax.all_gather(w_qkv, 'group', axis=0, tiled=True)]
    all_gather x1, waiting for transfers between devices: 125 us -> 86 us  [per_device(): lax.all_gather(w_fc, 'group', axis=0, tiled=True)]
    gather x0 -> x4, local copies, waits for them, and re-layouts: none -> 26.5 us  [_spread_yards(): vec_out = vec_out[(jnp.arange(chips) - step_out) % chips]]
    all_gather x1, waiting for transfers between devices: 25.2 us -> 0.01 us  [per_device(): lax.all_gather(w_out, 'group', axis=0, tiled=True)]
  transfers between devices with their start and end apart: 10 -> 13, of which waited for: 10 -> 8; matrix products, arithmetic and copies ran while one was open for 6% -> 8% of each run, Pallas kernels for 0% -> 0%
where the time goes in v1:
time: 2450 us; the launch traced here: 2440 us
  waiting for transfers between devices  1990 us (81%)
  blocking collectives  168 us (7%)
  matrix products  151 us (6%)
  local copies, waits for them, and re-layouts  63.4 us (3%)
  other arithmetic  40.1 us (2%)
    psum x1, waiting for transfers between devices, per_device(): lax.psum((owned[0], owned[1], owned[2], owned[3], owned[4], owned[5], own...  875 us
    reduce_scatter x1, waiting for transfers between devices, per_device(): lax.psum_scatter(grads[8], 'group', scatter_dimension=0, tiled=True)  296 us
    reduce_scatter x1, waiting for transfers between devices, per_device(): lax.psum_scatter(grads[10], 'group', scatter_dimension=0, tiled=True)  289 us
    reduce_scatter x1, waiting for transfers between devices, per_device(): lax.psum_scatter(grads[2], 'group', scatter_dimension=0, tiled=True)  224 us
    ppermute x2, waiting for transfers between devices, _spread_yards(): lax.ppermute(met_up[-1] if met_up else xx, axis_name=axis_tag, perm=nodes)  192 us
    unnamed x1, blocking collectives  129 us
    all_gather x1, waiting for transfers between devices, per_device(): lax.all_gather(w_fc, 'group', axis=0, tiled=True)  86 us
    dot_general x4, matrix products, matmul_left(): lax.dot_general(left_side, right_side, (((0,), (0,)), ((), ())), preferre...  56.4 us
  transfers between devices with their start and end apart: 13, of which 8 were waited for; matrix products, arithmetic and copies ran while one was open for 8% of the time, Pallas kernels for 0%

profile of v1, /device:TPU:0, one launch (start us, length us, event | category | flops | bytes accessed | tf_op | source)
XLA Modules:
  0.0 2441.6 jit_solution(11339359754468329954)
XLA Ops:
  10.7 2.0 collective-permute-start.2
  12.7 192.0 %collective-permute-done = bf16[400,6400]{1,0:T(8,128)(2,1)} collective-permute-done((bf16[400,6400]{1,0:T(8,128)(2,1)}, bf16[400,6400]{1,0:T(8,128)(2,1)}, u32[]{:S(2)}, u32[]{:S(2)}) %collective-permute-start) | collective-permute-done | bytes 5120032 | tf_op jit(solution)/shard_map/ppermute | solution.py:27
  204.7 4.4 collective-permute-start.1
  213.7 128.5 %all-reduce.19 = (bf16[3200]{0:T(1024)(128)(2,1)S(1)}, bf16[1600]{0:T(1024)(128)(2,1)S(1)}, bf16[1600]{0:T(1024)(128)(2,1)S(1)}, bf16[1600]{0:T(1024)(128)(2,1)S...) all-reduce(bf16[3200]{0:T(1024)(128)(2,1)S(1)} %dynamic-update-slic, ...), channel_id=1, replica_groups=mesh['group'=4,'replica'=8] {'group'}, use_global_device_ids=true, to_apply=%add.2 | all-reduce | flops 19200 | bytes 76800
  343.1 6.7 pad_maximum_fusion.2
  349.8 6.6 gather_fusion.2
  356.4 10.0 pad_maximum_fusion
  366.4 5.6 fusion.63
  371.9 7.2 gather_fusion.1
  379.1 7.2 gather_fusion
  386.3 16.8 pad_maximum_fusion.1
  403.1 13.4 fusion
  416.5 1.7 fusion.65
  418.5 2.3 fusion.66
  420.9 5.9 fusion.67
  427.0 14.2 convolution_add_fusion
  441.2 13.1 fusion.68
  454.2 86.0 %all-gather.11.cloned.1.call-done = bf16[1600,6400]{1,0:T(8,128)(2,1)} async-done(((bf16[400,6400]{1,0:T(8,128)(2,1)}), bf16[1600,6400]{1,0:T(8,128)(2,1)}) %all-gather.11.cloned.1.call-update) | async-done | bytes 20480016 | tf_op jit(solution)/shard_map/all_gather | solution.py:315
  540.2 12.6 multiply_reduce_fusion
  552.8 1.3 fusion.62
  554.1 0.9 copy-done.1
  555.0 5.7 fusion.55
  561.2 4.4 convolution_convert_fusion
  568.1 0.9 copy-done.4
  569.3 14.9 fusion.39
  584.3 0.9 copy-done.13
  585.2 19.0 fusion.42
  604.4 1.2 copy-done.3
  605.6 16.8 fusion.34
  622.5 1.1 copy-done.5
  623.8 1.3 pad_maximum_fusion.3
  626.4 9.8 fusion.27
  636.2 10.1 reduce-scatter.7.cloned.1.call-done
  646.3 224.2 %reduce-scatter.5.cloned.1.call-done = f32[400,4800]{1,0:T(8,128)} async-done(((f32[1600,4800]{1,0:T(8,128)}), f32[400,4800]{1,0:T(8,128)}) %reduce-scatter.5.cloned.1.call-update) | async-done | bytes 7680016 | tf_op jit(solution)/shard_map/reduce_scatter | solution.py:324
  870.5 289.3 %reduce-scatter.11.cloned.1.call-done = f32[1600,1600]{1,0:T(8,128)} async-done(((f32[6400,1600]{1,0:T(8,128)}), f32[1600,1600]{1,0:T(8,128)}) %reduce-scatter.11.cloned.1.call-update) | async-done | bytes 10240016 | tf_op jit(solution)/shard_map/reduce_scatter | solution.py:332
  1159.8 295.6 %reduce-scatter.9.cloned.1.call-done = f32[400,6400]{1,0:T(8,128)} async-done(((f32[1600,6400]{1,0:T(8,128)}), f32[400,6400]{1,0:T(8,128)}) %reduce-scatter.9.cloned.1.call-update) | async-done | bytes 10240016 | tf_op jit(solution)/shard_map/reduce_scatter | solution.py:330
  1458.1 1.2 fusion.26
  1459.2 14.8 fusion.9
  1474.0 17.7 all-reduce.25.cloned.1.call-done
  1491.7 0.8 dynamic-slice.9
  1492.5 0.8 dynamic-slice.11
  1497.1 0.8 dynamic-slice.21
  1497.9 39.9 %all-reduce.16 = (f32[400]{0:T(512)}, f32[400]{0:T(512)}, f32[800]{0:T(1024)}, f32[400]{0:T(512)}, f32[400]{0:T(512)}, /*index=5*/f32[400]{0:T(512)}, f32[1600]{0:T(1024)}, f32[400]{0:T(512)}) all-reduce(f32[400]{0:T(512)S(1)} %dynamic-slice.9, f32[400]{0:T(512)S(1)} %dynamic-slice.11, ...), channel_id=1, replica_groups=mesh['group'=4,'replica'=8] {'replica'}, use_global_device_ids=true, to_apply=%region_13.14 | all-reduce | flops 4800 | bytes 38400 | tf_op jit(solution)/shard_map/psum | solution.py:335
  1537.8 874.7 %all-reduce.23.cloned.1.call-done = (f32[400,4800]{1,0:T(8,128)}, f32[400,1600]{1,0:T(8,128)}, f32[400,6400]{1,0:T(8,128)}, f32[1600,1600]{1,0:T(8,128)}) async-done(((f32[400,4800]{1,0:T(8,128)}, f32[400,1600]{1,0:T(8,128)}, f32[400,6400]{1,0:T(8,128)}, f32[1600,1600]{1,0:T(8,128)}), (f32[400,4800]{1,0:T(8,128)}, f32[400,1600]{1,0:T(8,128)}, f32[400,6400]{1,0:T(8,128)}, ...) | async-done | bytes 30720016 | tf_op jit(solution)/shard_map/psum | solution.py:335
  2412.5 7.1 copy.64
  2419.6 1.5 copy.65
  2421.1 9.3 copy.66
  2430.4 4.1 copy.67
  (133 shorter events, 17.0 us)
Async XLA Ops:
  7.2 395.9 %all-gather.5.cloned.1.call-start = ((), (), s32[]{:S(2)}) async-start(), calls=%async_computation.4 | async-start | bytes 19456000 | tf_op jit(solution)/shard_map/all_gather | solution.py:294
  7.9 413.0 %all-gather.7.cloned.1.call-start = ((), (), s32[]{:S(2)}) async-start(), calls=%async_computation.5 | async-start | bytes 6656000 | tf_op jit(solution)/shard_map/all_gather | solution.py:296
  8.7 432.5 %all-gather.9.cloned.1.call-start = ((), (), s32[]{:S(2)}) async-start(), calls=%async_computation.6 | async-start | bytes 26624000 | tf_op jit(solution)/shard_map/all_gather | solution.py:302
  9.4 199.7 %copy-start.17 = (u32[32]{0:T(128)S(1)}, u32[32]{0:T(128)}, u32[]{:S(2)}) copy-start(u32[32]{0:T(128)} %constant.61) | copy-start | bytes 388
  9.4 202.2 %copy-start.19 = (bf16[400]{0:T(512)(128)(2,1)S(1)}, bf16[400]{0:T(512)(128)(2,1)}, u32[]{:S(2)}) copy-start(bf16[400]{0:T(512)(128)(2,1)} %param.19) | copy-start | bytes 2404
  9.4 202.5 %copy-start.20 = (bf16[400]{0:T(512)(128)(2,1)S(1)}, bf16[400]{0:T(512)(128)(2,1)}, u32[]{:S(2)}) copy-start(bf16[400]{0:T(512)(128)(2,1)} %param.18) | copy-start | bytes 2404
  9.4 202.7 %copy-start.21 = (bf16[400]{0:T(512)(128)(2,1)S(1)}, bf16[400]{0:T(512)(128)(2,1)}, u32[]{:S(2)}) copy-start(bf16[400]{0:T(512)(128)(2,1)} %param.23) | copy-start | bytes 2404
  9.4 203.0 %copy-start.22 = (bf16[400]{0:T(512)(128)(2,1)S(1)}, bf16[400]{0:T(512)(128)(2,1)}, u32[]{:S(2)}) copy-start(bf16[400]{0:T(512)(128)(2,1)} %param.29) | copy-start | bytes 2404
  9.5 203.2 %copy-start.23 = (bf16[400]{0:T(512)(128)(2,1)S(1)}, bf16[400]{0:T(512)(128)(2,1)}, u32[]{:S(2)}) copy-start(bf16[400]{0:T(512)(128)(2,1)} %param.25) | copy-start | bytes 2404
  9.5 203.5 %copy-start.24 = (bf16[400]{0:T(512)(128)(2,1)S(1)}, bf16[400]{0:T(512)(128)(2,1)}, u32[]{:S(2)}) copy-start(bf16[400]{0:T(512)(128)(2,1)} %param.24) | copy-start | bytes 2404
  9.5 203.7 %copy-start.18 = (bf16[800]{0:T(1024)(128)(2,1)S(1)}, bf16[800]{0:T(1024)(128)(2,1)}, u32[]{:S(2)}) copy-start(bf16[800]{0:T(1024)(128)(2,1)} %param.21) | copy-start | bytes 4804
  9.5 204.0 %copy-start.15 = (bf16[1600]{0:T(1024)(128)(2,1)S(1)}, bf16[1600]{0:T(1024)(128)(2,1)}, u32[]{:S(2)}) copy-start(bf16[1600]{0:T(1024)(128)(2,1)} %param.27) | copy-start | bytes 9604
  9.5 333.0 %copy-start = (bf16[1,128,1600]{1,2,0:T(8,128)(2,1)S(1)}, bf16[1,128,1600]{1,2,0:T(8,128)(2,1)}, u32[]{:S(2)}) copy-start(bf16[1,128,1600]{1,2,0:T(8,128)(2,1)} %param.15) | copy-start | bytes 1228804
  9.5 333.5 %copy-start.16 = (s32[1,128]{1,0:T(1,128)S(1)}, s32[1,128]{1,0:T(1,128)}, u32[]{:S(2)}) copy-start(s32[1,128]{1,0:T(1,128)} %param.16) | copy-start | bytes 1540
  9.5 530.7 %all-gather.11.cloned.1.call-start = ((), (), s32[]{:S(2)}) async-start(), calls=%async_computation.7 | async-start | bytes 25600000 | tf_op jit(solution)/shard_map/all_gather | solution.py:315
  10.1 636.2 %reduce-scatter.7.cloned.1.call-start = ((), (), s32[]{:S(2)}) async-start(), calls=%async_computation.9 | async-start | bytes 13312000 | tf_op jit(solution)/shard_map/reduce_scatter | solution.py:326
  10.1 194.6 %collective-permute-start = (bf16[400,6400]{1,0:T(8,128)(2,1)}, bf16[400,6400]{1,0:T(8,128)(2,1)}, u32[]{:S(2)}, u32[]{:S(2)}) collective-permute-start(bf16[400,6400]{1,0:T(8,128)(2,1)} %param.26), channel_id=1, source_target_pairs={{0,8},{8,16},{16,24},{24,0},{1,9},{9,17},{17,25},{25,1},{2,10},{10... | collective-permute-start | bytes 15360008 | tf_op jit(solution)/shard_map/ppermute | solution.py:27
  10.7 332.4 %collective-permute-start.2 = (bf16[400,6400]{1,0:T(8,128)(2,1)}, bf16[400,6400]{1,0:T(8,128)(2,1)}, u32[]{:S(2)}, u32[]{:S(2)}) collective-permute-start(bf16[400,6400]{1,0:T(8,128)(2,1)} %param.26), channel_id=1, source_target_pairs={{8,0},{16,8},{24,16},{0,24},{9,1},{17,9},{25,17},{1,25},{10,2},{18... | collective-permute-start | bytes 15360008 | tf_op jit(solution)/shard_map/ppermute | solution.py:30
  204.7 138.4 %collective-permute-start.1 = (bf16[400,6400]{1,0:T(8,128)(2,1)}, bf16[400,6400]{1,0:T(8,128)(2,1)}, u32[]{:S(2)}, u32[]{:S(2)}) collective-permute-start(bf16[400,6400]{1,0:T(8,128)(2,1)} %collective-permute-done), channel_id=1, source_target_pairs={{0,8},{8,16},{16,24},{24,0},{1,9},{9,17},{17,25},{25,1},{2,10},{10... | collective-permute-start | bytes 15360008 | tf_op jit(solution)/shard_map/ppermute | solution.py:27
  540.2 12.6 copy-start.12
  554.1 0.9 copy-start.1
  560.7 309.8 %reduce-scatter.5.cloned.1.call-start = ((), (), s32[]{:S(2)}) async-start(), calls=%async_computation.8 | async-start | bytes 38912000 | tf_op jit(solution)/shard_map/reduce_scatter | solution.py:324
  561.2 4.4 copy-start.10
  561.2 4.6 copy-start.9
  567.0 2.2 copy-start.6
  567.4 1.9 copy-start.8
  568.1 0.9 copy-start.4
  584.2 1.0 copy-start.13
  584.2 575.6 %reduce-scatter.11.cloned.1.call-start = ((), (), s32[]{:S(2)}) async-start(), calls=%async_computation.11 | async-start | bytes 53248000 | tf_op jit(solution)/shard_map/reduce_scatter | solution.py:332
  604.2 1.5 copy-start.3
  604.2 851.2 %reduce-scatter.9.cloned.1.call-start = ((), (), s32[]{:S(2)}) async-start(), calls=%async_computation.10 | async-start | bytes 51200000 | tf_op jit(solution)/shard_map/reduce_scatter | solution.py:330
  622.4 1.1 copy-start.5
  622.4 1.4 copy-start.7
  622.5 869.3 %all-reduce.25.cloned.1.call-start = ((), (), s32[]{:S(2)}) async-start(), calls=%async_computation.13 | async-start | bytes 188416
  636.1 1776.4 %all-reduce.23.cloned.1.call-start = ((), (), s32[]{:S(2)}) async-start(), calls=%async_computation.12 | async-start | bytes 62668800 | tf_op jit(solution)/shard_map/psum | solution.py:335
  1455.4 0.7 copy-start.14
  1455.4 2.7 copy-start.2
  2412.5 7.1 copy-start.11
  2419.6 10.8 slice-start
  2421.1 9.3 slice-start.1
  2421.1 9.3 slice-start.2
Sparse Core Ops, SparseCore 0:
  9.5 185.2 all-gather.4
  196.4 55.2 all-gather.6
  253.2 154.5 all-gather.8
  409.3 130.8 all-gather.10
  560.8 85.4 reduce-scatter.6
  648.8 221.6 reduce-scatter.4
  873.1 286.6 reduce-scatter.10
  1162.4 292.9 reduce-scatter.8
  1459.4 32.3 all-reduce.24
  1496.4 916.0 all-reduce.22
